TPU v7x, 1024 devices: a whole 8x8x8 slice. The times are simulated.
1024 devices in a mesh: row: 16 (over x, z_hi), col: 64 (over y, z_lo, core).
Axes of the slice: x: 8, y: 8, z: 8 (z_hi: 2, z_lo: 4; z = z_hi * 4 + z_lo), core: 2. Of those that a mesh axis runs over, the one named last changes fastest.
Arguments:
- pair_states: bfloat16 [1024, 16384], P(None, ('row', 'col')), may hold values from -0.046875 to 0.046875
- screening: bfloat16 [4, 16384, 16384], P(None, 'row', 'col'), may hold values from -6 to 6
- qp_energy: float32 [8], replicated, may hold values from -0.5 to 0.5
- band_energy: float32 [2048], replicated, may hold values from -2 to 2
- band_index: int32 [128], replicated, may hold values from 0 to 2047
- nodes: float32 [4], replicated, may hold values from 0.1 to 2
- node_weights: float32 [4], replicated, may hold values from 0.05 to 1
Outputs:
- contrib: float32 [8, 128], replicated
- sigma: float32 [8], replicated
All inputs are finite; a program needn't handle non-finite values.
Results may differ from a plain program's by a relative error of at most 0.0003.
Values may be sent and summed in bfloat16 or wider, within the bound.
No kernel may reach another device: no remote copies, remote signals or barrier semaphores. Data moves between devices by JAX's collectives and lax.ppermute only.
A program may use at most 64 MiB of HBM per device.

v0:
```python
import jax
import jax.numpy as jnp
from jax import lax
from jax.sharding import Mesh
from jax.sharding import PartitionSpec as P

COL = ("col_0", "col_1", "col_2")
ROW = ("row_0", "row_1")
ROW_COL = ("row_0", "row_1", "col_0", "col_1", "col_2")


def in_order(pieces, dim):
    pieces = jnp.moveaxis(pieces, 0, dim)
    shape = pieces.shape
    return pieces.reshape(*shape[:dim], shape[dim] * shape[dim + 1], *shape[dim + 2 :])


def sent_to_all(array, axis):
    copies = jnp.broadcast_to(array, (lax.axis_size(axis), *array.shape))
    return lax.all_to_all(copies, axis, split_axis=0, concat_axis=0, tiled=True)


def gather_directly(array, axis, dim):
    return in_order(sent_to_all(array, axis), dim)


def from_root(array, axes, root):
    array = jnp.where(lax.axis_index(axes) == root, array, jnp.zeros_like(array))
    for axis in axes:
        array = lax.psum(array, axis)
    return array


def over_axes(array, axes):
    for axis in axes:
        array = lax.psum(array, axis)
    return array


def shards(pair_states, screening, qp_energy, band_energy, band_index, nodes, node_weights):
    width = screening.shape[2]
    panel = gather_directly(pair_states, COL, 1)
    images = jnp.einsum("pg,fgc->fpc", panel, screening, preferred_element_type=jnp.float32)
    ratio = lax.axis_size(COL) // lax.axis_size(ROW)
    column = lax.axis_index(COL)
    offset = column % ratio * width
    own_piece = lax.dynamic_slice_in_dim(panel, offset, width, 1)
    col_states = from_root(own_piece, ROW, column // ratio)
    partial_value = jnp.sum(images * col_states.astype(jnp.float32)[None, :, :], axis=2)
    table = lax.broadcasted_iota(jnp.int32, (band_index.shape[0], band_energy.shape[0]), 1)
    chosen = jnp.sum(
        jnp.where(band_index[:, None] == table, band_energy[None, :], jnp.float32(0.0)), axis=1
    )
    gap = (qp_energy[:, None] - chosen[None, :]).reshape(-1)
    factor = (
        node_weights[:, None]
        * gap[None, :]
        / (gap[None, :] * gap[None, :] + nodes[:, None] * nodes[:, None])
    )
    flat = over_axes(jnp.sum(factor * partial_value, axis=0), ROW_COL)
    contrib = flat.reshape(qp_energy.shape[0], band_index.shape[0])
    sigma = jnp.sum(contrib, axis=1)
    return (contrib, sigma)


def solution(mesh):
    split = Mesh(mesh.devices.reshape(8, 2, 8, 4, 2), ("row_0", "row_1", "col_0", "col_1", "col_2"))
    return jax.shard_map(
        shards,
        mesh=split,
        in_specs=(P(None, ROW_COL), P(None, ROW, COL), P(), P(), P(), P(), P()),
        out_specs=(P(), P()),
        check_vma=False,
    )
```

profile of v0, /device:TPU:1, one launch (start us, length us, event | category | flops | bytes accessed | tf_op | source)
XLA Modules:
  0.0 306.7 jit_solution(8632431720676994896)
XLA Ops:
  7.2 0.0 copy-start
  7.2 2.5 broadcast_in_dim.28
  9.6 0.0 copy-start.6
  9.6 19.2 %all-to-all-start = ((bf16[64,1024,16]{1,2,0:T(8,128)(2,1)}), bf16[64,1024,16]{1,2,0:T(8,128)(2,1)}, u32[]{:S(2)}, u32[]{:S(2)}) async-start(bf16[64,1024,16]{1,2,0:T(8,128)(2,1)} %broadcast_in_dim.28), calls=%async_computation | async-start | bytes 4194304 | tf_op jit(solution)/shard_map/all_to_all | solution.py:20
  28.8 0.0 copy-start.2
  28.8 0.0 copy-start.4
  28.8 0.0 copy-start.3
  28.9 0.0 all-reduce.3.cloned.1.call-start
  28.9 50.4 %all-to-all-done = bf16[64,1024,16]{1,2,0:T(8,128)(2,1)} async-done(((bf16[64,1024,16]{1,2,0:T(8,128)(2,1)}), bf16[64,1024,16]{1,2,0:T(8,128)(2,1)}, u32[]{:S(2)}, u32[]{:S(2)}) %all-to-all-start) | async-done | bytes 2097184 | tf_op jit(solution)/shard_map/all_to_all | solution.py:20
  79.3 2.0 dynamic-slice_select_fusion
  81.3 0.0 all-reduce.3.cloned.1.call-update
  81.3 0.0 all-reduce.5.cloned.1.call-start
  81.3 0.0 copy-done.6
  81.4 81.7 %all-reduce.3.cloned.1.call-done = bf16[1024,256]{0,1:T(8,128)(2,1)} async-done(((bf16[1024,256]{0,1:T(8,128)(2,1)}), bf16[1024,256]{0,1:T(8,128)(2,1)}) %all-reduce.3.cloned.1.call-update) | async-done | bytes 524304 | tf_op jit(solution)/shard_map/psum | solution.py:30
  163.1 0.0 all-reduce.5.cloned.1.call-update
  163.1 0.0 copy-done.2
  163.1 0.0 copy-done.4
  163.1 0.3 select_reduce_fusion
  163.4 0.0 copy-done.3
  163.4 0.1 fusion.1
  163.4 0.1 subtract_bitcast_fusion
  163.5 75.1 %all-reduce.5.cloned.1.call-done = bf16[1024,256]{0,1:T(8,128)(2,1)} async-done(((bf16[1024,256]{0,1:T(8,128)(2,1)}), bf16[1024,256]{0,1:T(8,128)(2,1)}) %all-reduce.5.cloned.1.call-update) | async-done | bytes 524304 | tf_op jit(solution)/shard_map/psum | solution.py:30
  238.6 1.1 convert_element_type.3
  239.8 0.0 copy-done
  239.8 0.0 copy-start.5
  239.8 4.1 %fusion = f32[4,1024]{1,0:T(4,128)S(1)} fusion(bf16[4,1024,256]{2,1,0:T(8,128)(2,1)S(1)} %copy-done, bf16[1024,1024,1]{0,1,2:T(8,128)(2,1)} %bitcast.3, f32[1024,256]{0,1:T(8,128)S(1)} %convert_element_type.3), kind=kOutput, calls=%fused_computation.1 | convolution fusion | flops 2149576704 | bytes 5259264 | tf_op jit(solution)/shard_map/pg,fgc->fpc/dot_general | solution.py:43
  243.9 0.0 copy-done.5
  243.9 0.1 multiply_reduce_fusion
  244.0 13.2 %psum.51 = f32[1024]{0:T(1024)S(1)} all-reduce(f32[1024]{0:T(1024)S(1)} %multiply_reduce_fusion), channel_id=1, replica_groups=mesh['row_0'=8,'row_1'=2,'col_0'=8,'col_1'=4,'col_2'=2] {'row_0'}, use_global_device_ids=true, to_apply=%region_5.6 | all-reduce | flops 1024 | bytes 8192 | tf_op jit(solution)/shard_map/psum | solution.py:36
  257.1 7.7 %psum.52 = f32[1024]{0:T(1024)S(1)} all-reduce(f32[1024]{0:T(1024)S(1)} %psum.51), channel_id=1, replica_groups=mesh['row_0'=8,'row_1'=2,'col_0'=8,'col_1'=4,'col_2'=2] {'row_1'}, use_global_device_ids=true, to_apply=%region_6.7 | all-reduce | flops 1024 | bytes 8192 | tf_op jit(solution)/shard_map/psum | solution.py:36
  264.8 13.7 %psum.53 = f32[1024]{0:T(1024)S(1)} all-reduce(f32[1024]{0:T(1024)S(1)} %psum.52), channel_id=1, replica_groups=mesh['row_0'=8,'row_1'=2,'col_0'=8,'col_1'=4,'col_2'=2] {'col_0'}, use_global_device_ids=true, to_apply=%region_7.8 | all-reduce | flops 1024 | bytes 8192 | tf_op jit(solution)/shard_map/psum | solution.py:36
  278.5 7.3 %psum.54 = f32[1024]{0:T(1024)S(1)} all-reduce(f32[1024]{0:T(1024)S(1)} %psum.53), channel_id=1, replica_groups=mesh['row_0'=8,'row_1'=2,'col_0'=8,'col_1'=4,'col_2'=2] {'col_1'}, use_global_device_ids=true, to_apply=%region_8.9 | all-reduce | flops 1024 | bytes 8192 | tf_op jit(solution)/shard_map/psum | solution.py:36
  285.8 13.4 %psum.55 = f32[8,128]{1,0:T(8,128)S(1)} all-reduce(f32[8,128]{1,0:T(8,128)S(1)} %bitcast.16), channel_id=1, replica_groups=mesh['row_0'=8,'row_1'=2,'col_0'=8,'col_1'=4,'col_2'=2] {'col_2'}, use_global_device_ids=true, to_apply=%region_9.10 | all-reduce | flops 1024 | bytes 8192 | tf_op jit(solution)/shard_map/psum | solution.py:36
  299.2 0.0 copy-start.1
  299.2 0.6 reduce_sum.39
  299.8 0.0 copy-done.1
  (1 shorter events, 0.0 us)
Async XLA Ops:
  7.2 232.6 %copy-start = (bf16[4,1024,256]{2,1,0:T(8,128)(2,1)S(1)}, bf16[4,1024,256]{2,1,0:T(8,128)(2,1)}, u32[]{:S(2)}) copy-start(bf16[4,1024,256]{2,1,0:T(8,128)(2,1)} %param.8) | copy-start | bytes 6291460
  9.6 71.7 %copy-start.6 = (f32[4]{0:T(128)S(1)}, f32[4]{0:T(128)}, u32[]{:S(2)}) copy-start(f32[4]{0:T(128)} %param.12) | copy-start | bytes 52
  9.6 69.7 %all-to-all-start = ((bf16[64,1024,16]{1,2,0:T(8,128)(2,1)}), bf16[64,1024,16]{1,2,0:T(8,128)(2,1)}, u32[]{:S(2)}, u32[]{:S(2)}) async-start(bf16[64,1024,16]{1,2,0:T(8,128)(2,1)} %broadcast_in_dim.28), calls=%async_computation | async-start | bytes 4194304 | tf_op jit(solution)/shard_map/all_to_all | solution.py:20
  28.8 134.3 %copy-start.2 = (f32[2048]{0:T(1024)S(1)}, f32[2048]{0:T(1024)}, u32[]{:S(2)}) copy-start(f32[2048]{0:T(1024)} %param.10) | copy-start | bytes 24580
  28.8 134.3 %copy-start.4 = (s32[128]{0:T(128)S(1)}, s32[128]{0:T(128)}, u32[]{:S(2)}) copy-start(s32[128]{0:T(128)} %param.11) | copy-start | bytes 1540
  28.8 134.5 %copy-start.3 = (f32[8]{0:T(128)S(1)}, f32[8]{0:T(128)}, u32[]{:S(2)}) copy-start(f32[8]{0:T(128)} %param.9) | copy-start | bytes 100
  28.9 134.2 %all-reduce.3.cloned.1.call-start = ((), (), s32[]{:S(2)}) async-start(), calls=%async_computation.1 | async-start | bytes 1048576 | tf_op jit(solution)/shard_map/psum | solution.py:30
  81.3 157.3 %all-reduce.5.cloned.1.call-start = ((), (), s32[]{:S(2)}) async-start(), calls=%async_computation.2 | async-start | bytes 1048576 | tf_op jit(solution)/shard_map/psum | solution.py:30
  239.8 4.1 %copy-start.5 = (f32[4]{0:T(128)S(1)}, f32[4]{0:T(128)}, u32[]{:S(2)}) copy-start(f32[4]{0:T(128)} %param.13) | copy-start | bytes 52
  299.2 0.6 copy-start.1
Sparse Core Ops, SparseCore 0:
  81.4 81.6 all-reduce.2
  166.5 72.0 all-reduce.4
where the time goes:
time: 307 us
  waiting for transfers between devices  207 us (67%)
  blocking collectives  55.2 us (18%)
  starting transfers between devices  19.2 us (6%)
  between operations  14.2 us (5%)
  other arithmetic  4.21 us (1%)
  matrix products  4.05 us (1%)
    psum x2, waiting for transfers between devices, from_root(): array = lax.psum(array, axis)  157 us
    psum x5, blocking collectives, over_axes(): array = lax.psum(array, axis)  55.2 us
    all_to_all x1, waiting for transfers between devices, sent_to_all(): return lax.all_to_all(copies, axis, split_axis=0, concat_axis=0, tiled=True)  50.4 us
    all_to_all x1, starting transfers between devices, sent_to_all(): return lax.all_to_all(copies, axis, split_axis=0, concat_axis=0, tiled=True)  19.2 us
  transfers between devices with their start and end apart: 3, of which 3 were waited for; matrix products, arithmetic and copies ran while one was open for 0% of the time, Pallas kernels for 0%

commit v1 on v0

v1 whole, which is shorter than its diff:
```python
import jax
import jax.numpy as jnp
from jax import lax
from jax.experimental import pallas as pl
from jax.experimental.pallas import tpu as pltpu
from jax.sharding import Mesh
from jax.sharding import PartitionSpec as P

AXES = ("x", "zh", "y", "zl", "core")
SIZES = (8, 2, 8, 4, 2)
ROW = ("x", "zh")
COL = ("y", "zl", "core")
VMEM = pl.BlockSpec(memory_space=pltpu.VMEM)


def sent_to_all(array, axes):
    copies = jnp.broadcast_to(array, (lax.axis_size(axes), *array.shape))
    return lax.all_to_all(copies, axes, split_axis=0, concat_axis=0, tiled=True)


def transposed_place():
    return [(b, (b % 16) * 64 + b // 16) for b in range(1024)]


def weigh(has_base, w_ref, row_ref, factor_ref, *refs):
    out_ref = refs[-1]
    for k in range(0, 1024, 256):
        states = row_ref[:, k : k + 256]
        total = refs[0][:, k : k + 256] if has_base else None
        for f in range(4):
            image = jnp.dot(w_ref[f], states, preferred_element_type=jnp.float32)
            term = image * factor_ref[f : f + 1, k : k + 256]
            total = term if total is None else total + term
        out_ref[:, k : k + 256] = total


def weighed(w, row, factor, *base):
    return pl.pallas_call(
        lambda *refs: weigh(len(base) > 0, *refs),
        out_shape=jax.ShapeDtypeStruct((256, 1024), jnp.float32),
        in_specs=[VMEM] * (3 + len(base)),
        out_specs=VMEM,
        cost_estimate=pl.CostEstimate(flops=2 * 4 * 512 * 256 * 1024, bytes_accessed=4 << 20, transcendentals=0),
    )(w, row, factor, *base)


def project(weighed_ref, col_ref, out_ref):
    for n in range(8):
        part = slice(n * 128, n * 128 + 128)
        total = jnp.sum(weighed_ref[:, part] * col_ref[:, part].astype(jnp.float32), axis=0, keepdims=True)
        for copy in range(out_ref.shape[0]):
            out_ref[copy, n : n + 1, :] = total


def add(pieces_ref, out_ref):
    total = pieces_ref[0]
    for piece in range(1, pieces_ref.shape[0]):
        total = total + pieces_ref[piece]
    for copy in range(out_ref.shape[0]):
        out_ref[copy] = total


def in_kernel(body, copies, *args):
    return pl.pallas_call(
        body,
        out_shape=jax.ShapeDtypeStruct((copies, 8, 128), jnp.float32),
        in_specs=[VMEM] * len(args),
        out_specs=VMEM,
    )(*args)


def exchanged(copies, axes):
    return lax.all_to_all(copies, axes, split_axis=0, concat_axis=0, tiled=True)


def factors(qp_energy, band_energy, band_index, nodes, node_weights):
    table = lax.broadcasted_iota(jnp.int32, (band_index.shape[0], band_energy.shape[0]), 1)
    chosen = jnp.sum(
        jnp.where(band_index[:, None] == table, band_energy[None, :], jnp.float32(0.0)), axis=1
    )
    gap = (qp_energy[:, None] - chosen[None, :]).reshape(-1)
    return (
        node_weights[:, None]
        * gap[None, :]
        / (gap[None, :] * gap[None, :] + nodes[:, None] * nodes[:, None])
    )


def shards(pair_states, screening, qp_energy, band_energy, band_index, nodes, node_weights):
    piece = pair_states.T
    moved = lax.ppermute(piece, ROW + COL, transposed_place())
    factor = factors(qp_energy, band_energy, band_index, nodes, node_weights)
    core = lax.axis_index("core")
    slabs = screening.reshape(4, 32, 2, 16, 256)
    own_w, other_w = (
        lax.dynamic_index_in_dim(slabs, which, 2, keepdims=False).reshape(4, 512, 256).transpose(0, 2, 1)
        for which in (core, 1 - core)
    )
    row = sent_to_all(piece, ("y", "zl")).reshape(512, 1024)
    other = lax.ppermute(row, "core", [(0, 1), (1, 0)])
    col = sent_to_all(moved, ROW).reshape(256, 1024)
    weighted = weighed(own_w, row, factor)
    weighted = weighed(other_w, other, factor, weighted)
    copies = in_kernel(project, 16, weighted, col)
    copies = in_kernel(add, 64, exchanged(copies, ("zh", "zl", "core")))
    contrib = in_kernel(add, 1, exchanged(copies, ("x", "y")))[0]
    sigma = jnp.sum(contrib, axis=1)
    return (contrib, sigma)


def solution(mesh):
    split = Mesh(mesh.devices.reshape(SIZES), AXES)
    return jax.shard_map(
        shards,
        mesh=split,
        in_specs=(P(None, ROW + COL), P(None, ROW, COL), P(), P(), P(), P(), P()),
        out_specs=(P(), P()),
        check_vma=False,
    )
```

time: 307 us -> 139 us (0.45)
  waiting for transfers between devices: 207 us -> 28.5 us
  starting transfers between devices: 19.2 us -> 49.7 us
  blocking collectives: 55.2 us -> 35.3 us
  between operations: 14.2 us -> 0.76 us
  Pallas kernels: 0 us -> 13.2 us
  local copies, waits for them, and re-layouts: 2.5 us -> 8.07 us
  matrix products: 4.05 us -> 0 us
    psum x2 -> x0, waiting for transfers between devices: 157 us -> none  [from_root(): array = lax.psum(array, axis)]
    psum x5 -> x0, blocking collectives: 55.2 us -> none  [over_axes(): array = lax.psum(array, axis)]
    all_to_all x0 -> x2, blocking collectives: none -> 35.3 us  [exchanged(): return lax.all_to_all(copies, axes, split_axis=0, concat_axis=0, tiled=True)]
    all_to_all x1 -> x2, waiting for transfers between devices: 50.4 us -> 28.5 us  [sent_to_all(): return lax.all_to_all(copies, axes, split_axis=0, concat_axis=0, tiled=True)]
    ppermute x0 -> x2, starting transfers between devices: none -> 17.3 us  [the longest x1 12.4 us: shards(): moved = lax.ppermute(piece, ROW + COL, transposed_place())]
    all_to_all x1 -> x2, starting transfers between devices: 19.2 us -> 32.4 us  [sent_to_all(): return lax.all_to_all(copies, axes, split_axis=0, concat_axis=0, tiled=True)]
    pallas_call x0 -> x5, Pallas kernels: none -> 13.2 us  [the longest x2 7.91 us: weighed(): pl.pallas_call(lambda *refs: weigh(len(base) > 0, *refs), out_shape=jax.S...]
    dot_general x1 -> x0, matrix products: 4.05 us -> none  [shards(): jnp.einsum('pg,fgc->fpc', panel, screening, preferred_element_type=jnp.fl...]
  transfers between devices with their start and end apart: 3 -> 4, of which waited for: 3 -> 2; matrix products, arithmetic and copies ran while one was open for 0% -> 5% of each run, Pallas kernels for 0% -> 6%
where the time goes in v1:
time: 139 us; the launch traced here: 138 us
  starting transfers between devices  49.7 us (36%)
  blocking collectives  35.3 us (25%)
  waiting for transfers between devices  28.5 us (21%)
  Pallas kernels  13.2 us (9%)
  local copies, waits for them, and re-layouts  8.07 us (6%)
  other arithmetic  2.39 us (2%)
    all_to_all x2, blocking collectives, exchanged(): return lax.all_to_all(copies, axes, split_axis=0, concat_axis=0, tiled=True)  35.3 us
    all_to_all x2, starting transfers between devices, sent_to_all(): return lax.all_to_all(copies, axes, split_axis=0, concat_axis=0, tiled=True)  32.4 us
    all_to_all x2, waiting for transfers between devices, sent_to_all(): return lax.all_to_all(copies, axes, split_axis=0, concat_axis=0, tiled=True)  28.5 us
    ppermute x1, starting transfers between devices, shards(): moved = lax.ppermute(piece, ROW + COL, transposed_place())  12.4 us
    pallas_call x2, Pallas kernels, weighed(): pl.pallas_call(lambda *refs: weigh(len(base) > 0, *refs), out_shape=jax.S...  7.91 us
    pallas_call x3, Pallas kernels, in_kernel(): pl.pallas_call(body, out_shape=jax.ShapeDtypeStruct((copies, 8, 128), jnp...  5.31 us
    ppermute x1, starting transfers between devices, shards(): other = lax.ppermute(row, 'core', [(0, 1), (1, 0)])  4.85 us
    broadcast_in_dim x2, local copies, waits for them, and re-layouts, sent_to_all(): copies = jnp.broadcast_to(array, (lax.axis_size(axes), *array.shape))  2.79 us
  transfers between devices with their start and end apart: 4, of which 2 were waited for; matrix products, arithmetic and copies ran while one was open for 5% of the time, Pallas kernels for 6%

profile of v1, /device:TPU:1, one launch (start us, length us, event | category | flops | bytes accessed | tf_op | source)
XLA Modules:
  0.0 137.9 jit_solution(16121058163290079797)
XLA Ops:
  0.6 0.0 copy-start.2
  0.6 1.9 %broadcast_in_dim.16 = bf16[32,16,1024]{2,1,0:T(8,128)(2,1)} broadcast(bf16[16,1024]{1,0:T(8,128)(2,1)} %bitcast.21), dimensions={1,2} | broadcast | bytes 1081344 | tf_op jit(solution)/shard_map/broadcast_in_dim | solution.py:17
  2.5 16.6 %all-to-all-start = ((bf16[32,16,1024]{2,1,0:T(8,128)(2,1)}), bf16[32,16,1024]{2,1,0:T(8,128)(2,1)S(1)}, u32[]{:S(2)}, u32[]{:S(2)}) async-start(bf16[32,16,1024]{2,1,0:T(8,128)(2,1)} %broadcast_in_dim.16), calls=%async_computation | async-start | bytes 2097152 | tf_op jit(solution)/shard_map/all_to_all | solution.py:18
  19.2 0.0 copy-done.2
  19.2 12.4 %collective-permute-start.1 = (bf16[16,1024]{1,0:T(8,128)(2,1)S(1)}, bf16[16,1024]{1,0:T(8,128)(2,1)S(1)}, u32[]{:S(2)}, u32[]{:S(2)}) collective-permute-start(bf16[16,1024]{1,0:T(8,128)(2,1)S(1)} %bitcast.22), channel_id=1, source_target_pairs={{0,0},{1,64},{2,128},{3,192},{4,256},{5,320},{6,384},{7,448},{8,51... | collective-permute-start | bytes 98312 | tf_op jit(solution)/shard_map/ppermute | solution.py:91
  31.6 17.2 %all-to-all-done = bf16[32,16,1024]{2,1,0:T(8,128)(2,1)S(1)} async-done(((bf16[32,16,1024]{2,1,0:T(8,128)(2,1)}), bf16[32,16,1024]{2,1,0:T(8,128)(2,1)S(1)}, u32[]{:S(2)}, u32[]{:S(2)}) %all-to-all-start) | async-done | bytes 1048608 | tf_op jit(solution)/shard_map/all_to_all | solution.py:18
  48.8 0.0 copy-start.1
  48.8 4.9 %collective-permute-start = (bf16[512,1024]{1,0:T(8,128)(2,1)S(1)}, bf16[512,1024]{1,0:T(8,128)(2,1)}, u32[]{:S(2)}, u32[]{:S(2)}) collective-permute-start(bf16[512,1024]{1,0:T(8,128)(2,1)S(1)} %bitcast.18), channel_id=1, source_target_pairs={{0,1},{1,0},{2,3},{3,2},{4,5},{5,4},{6,7},{7,6},{8,9},{9,8},{10,11... | collective-permute-start | bytes 3145736 | tf_op jit(solution)/shard_map/ppermute | solution.py:100
  53.7 1.8 %constant_dynamic-slice_fusion = (bf16[4,32,1,16,256]{4,3,2,1,0:T(8,128)(2,1)S(1)}, bf16[4,32,1,16,256]{4,3,2,1,0:T(8,128)(2,1)S(1)}) fusion(bf16[4,32,2,16,256]{4,3,2,1,0:T(8,128)(2,1)} %bitcast.16, s32[]{:T(128)S(6)} %select_n.13, s32[]{:T(128)S(6)} %select_n.11), kind=kLoop, calls=%fused_computation.4 | loop fusion | bytes 4194312 | tf_op jit(solution)/shard_map/jit(dynamic_index_in_dim)/dynamic_slice | solution.py:96
  55.5 0.0 copy-done.1
  55.5 0.0 copy-start.7
  55.5 1.3 copy.16
  56.8 0.0 copy-done.7
  56.8 0.0 copy-start.3
  56.8 0.0 copy-start.5
  56.8 0.0 copy-start.4
  56.8 0.0 copy-start.6
  56.9 1.3 copy.15
  58.2 0.0 collective-permute-done.1
  58.2 0.9 broadcast_in_dim.28
  59.1 15.8 %all-to-all-start.1 = ((bf16[16,16,1024]{2,1,0:T(8,128)(2,1)}), bf16[16,16,1024]{2,1,0:T(8,128)(2,1)S(1)}, u32[]{:S(2)}, u32[]{:S(2)}) async-start(bf16[16,16,1024]{2,1,0:T(8,128)(2,1)} %broadcast_in_dim.28), calls=%async_computation.1 | async-start | bytes 1048576 | tf_op jit(solution)/shard_map/all_to_all | solution.py:18
  74.9 0.0 copy-done.3
  74.9 0.0 copy-done.5
  74.9 0.3 select_reduce_fusion
  75.1 0.0 copy-done.4
  75.1 0.1 fusion
  75.2 0.1 subtract_bitcast_fusion
  75.3 0.0 copy-done.6
  75.3 0.7 add_divide_fusion.refs_2_
  76.0 3.8 %shard_map.86.refs_3_ = f32[256,1024]{1,0:T(8,128)} custom-call(bf16[4,256,512]{2,1,0:T(8,128)(2,1)} %bitcast.20, bf16[512,1024]{1,0:T(8,128)(2,1)} %bitcast.19, f32[4,1024]{1,0:T(4,128)} %add_divide_fusion.refs_2_), custom_call_target="tpu_custom_call" | custom-call | flops 1073741824 | bytes 4194304 | tf_op jit(solution)/shard_map/pallas_call | solution.py:38
  79.8 0.0 collective-permute-done.refs_1_
  79.8 4.1 %shard_map.87.weighed_ref = f32[256,1024]{1,0:T(8,128)} custom-call(bf16[4,256,512]{2,1,0:T(8,128)(2,1)} %bitcast.15, bf16[512,1024]{1,0:T(8,128)(2,1)} %collective-permute-done.refs_1_, f32[4,1024]{1,0:T(4,128)} %add_divide_fusion.refs_2_, f32[256,1024]{1,0:T(8,128)} %shard_map.86.refs_3_), custom_call_target="tpu_custom_call" | custom-call | flops 1073741824 | bytes 4194304 | tf_op jit(solution)/shard_map/pallas_call | solution.py:38
  83.9 11.4 %all-to-all-done.1 = bf16[16,16,1024]{2,1,0:T(8,128)(2,1)S(1)} async-done(((bf16[16,16,1024]{2,1,0:T(8,128)(2,1)}), bf16[16,16,1024]{2,1,0:T(8,128)(2,1)S(1)}, u32[]{:S(2)}, u32[]{:S(2)}) %all-to-all-start.1) | async-done | bytes 524320 | tf_op jit(solution)/shard_map/all_to_all | solution.py:18
  95.2 0.0 copy-start
  95.2 0.8 copy-done
  96.0 2.1 %shard_map.88 = f32[16,8,128]{2,1,0:T(8,128)} custom-call(f32[256,1024]{1,0:T(8,128)} %shard_map.87.weighed_ref, bf16[256,1024]{1,0:T(8,128)(2,1)} %bitcast.17), custom_call_target="tpu_custom_call" | custom-call | tf_op jit(solution)/shard_map/pallas_call | solution.py:64
  98.2 14.1 %all_to_all.20.pieces_ref = f32[16,8,128]{2,1,0:T(8,128)} all-to-all(f32[16,8,128]{2,1,0:T(8,128)} %shard_map.88), channel_id=1, replica_groups=mesh['x'=8,'zh'=2,'y'=8,'zl'=4,'core'=2] {'zh','zl','core'}, dimensions={0} | all-to-all | bytes 131072 | tf_op jit(solution)/shard_map/all_to_all | solution.py:73
  112.3 1.6 %shard_map.89 = f32[64,8,128]{2,1,0:T(8,128)} custom-call(f32[16,8,128]{2,1,0:T(8,128)} %all_to_all.20.pieces_ref), custom_call_target="tpu_custom_call" | custom-call | tf_op jit(solution)/shard_map/pallas_call | solution.py:64
  113.8 21.2 %all_to_all.21.pieces_ref = f32[64,8,128]{2,1,0:T(8,128)} all-to-all(f32[64,8,128]{2,1,0:T(8,128)} %shard_map.89), channel_id=1, replica_groups=mesh['x'=8,'zh'=2,'y'=8,'zl'=4,'core'=2] {'x','y'}, dimensions={0} | all-to-all | bytes 524288 | tf_op jit(solution)/shard_map/all_to_all | solution.py:73
  135.0 1.6 %shard_map.90 = f32[1,8,128]{2,1,0:T(8,128)} custom-call(f32[64,8,128]{2,1,0:T(8,128)} %all_to_all.21.pieces_ref), custom_call_target="tpu_custom_call" | custom-call | tf_op jit(solution)/shard_map/pallas_call | solution.py:64
  136.6 1.3 reduce_sum.19
  (1 shorter events, 0.0 us)
Async XLA Ops:
  0.6 18.6 %copy-start.2 = (bf16[1024,16]{0,1:T(8,128)(2,1)S(1)}, bf16[1024,16]{0,1:T(8,128)(2,1)}, u32[]{:S(2)}) copy-start(bf16[1024,16]{0,1:T(8,128)(2,1)} %param.7) | copy-start | bytes 98308
  2.5 46.3 %all-to-all-start = ((bf16[32,16,1024]{2,1,0:T(8,128)(2,1)}), bf16[32,16,1024]{2,1,0:T(8,128)(2,1)S(1)}, u32[]{:S(2)}, u32[]{:S(2)}) async-start(bf16[32,16,1024]{2,1,0:T(8,128)(2,1)} %broadcast_in_dim.16), calls=%async_computation | async-start | bytes 2097152 | tf_op jit(solution)/shard_map/all_to_all | solution.py:18
  19.2 39.0 %collective-permute-start.1 = (bf16[16,1024]{1,0:T(8,128)(2,1)S(1)}, bf16[16,1024]{1,0:T(8,128)(2,1)S(1)}, u32[]{:S(2)}, u32[]{:S(2)}) collective-permute-start(bf16[16,1024]{1,0:T(8,128)(2,1)S(1)} %bitcast.22), channel_id=1, source_target_pairs={{0,0},{1,64},{2,128},{3,192},{4,256},{5,320},{6,384},{7,448},{8,51... | collective-permute-start | bytes 98312 | tf_op jit(solution)/shard_map/ppermute | solution.py:91
  48.8 6.7 %copy-start.1 = (bf16[32,16,1024]{2,1,0:T(8,128)(2,1)}, bf16[32,16,1024]{2,1,0:T(8,128)(2,1)S(1)}, u32[]{:S(2)}) copy-start(bf16[32,16,1024]{2,1,0:T(8,128)(2,1)S(1)} %all-to-all-done) | copy-start | bytes 3145732
  48.8 31.0 %collective-permute-start = (bf16[512,1024]{1,0:T(8,128)(2,1)S(1)}, bf16[512,1024]{1,0:T(8,128)(2,1)}, u32[]{:S(2)}, u32[]{:S(2)}) collective-permute-start(bf16[512,1024]{1,0:T(8,128)(2,1)S(1)} %bitcast.18), channel_id=1, source_target_pairs={{0,1},{1,0},{2,3},{3,2},{4,5},{5,4},{6,7},{7,6},{8,9},{9,8},{10,11... | collective-permute-start | bytes 3145736 | tf_op jit(solution)/shard_map/ppermute | solution.py:100
  55.5 1.3 copy-start.7
  56.8 18.0 %copy-start.3 = (f32[2048]{0:T(1024)S(1)}, f32[2048]{0:T(1024)}, u32[]{:S(2)}) copy-start(f32[2048]{0:T(1024)} %param.10) | copy-start | bytes 24580
  56.8 18.0 %copy-start.5 = (s32[128]{0:T(128)S(1)}, s32[128]{0:T(128)}, u32[]{:S(2)}) copy-start(s32[128]{0:T(128)} %param.11) | copy-start | bytes 1540
  56.8 18.3 %copy-start.4 = (f32[8]{0:T(128)S(1)}, f32[8]{0:T(128)}, u32[]{:S(2)}) copy-start(f32[8]{0:T(128)} %param.9) | copy-start | bytes 100
  56.8 18.4 %copy-start.6 = (f32[4]{0:T(128)S(1)}, f32[4]{0:T(128)}, u32[]{:S(2)}) copy-start(f32[4]{0:T(128)} %param.13) | copy-start | bytes 52
  59.1 36.2 %all-to-all-start.1 = ((bf16[16,16,1024]{2,1,0:T(8,128)(2,1)}), bf16[16,16,1024]{2,1,0:T(8,128)(2,1)S(1)}, u32[]{:S(2)}, u32[]{:S(2)}) async-start(bf16[16,16,1024]{2,1,0:T(8,128)(2,1)} %broadcast_in_dim.28), calls=%async_computation.1 | async-start | bytes 1048576 | tf_op jit(solution)/shard_map/all_to_all | solution.py:18
  95.2 0.8 copy-start
